TPU v7x, 16 devices: a whole 2x2x2 slice. The times are simulated.
16 devices in a mesh: data: 4 (over z, y), stage: 4 (over x, core).
Axes of the slice: x: 2, y: 2, z: 2, core: 2. Of those that a mesh axis runs over, the one named last changes fastest.
Arguments:
- x_in: bfloat16 [128, 256, 768], P('data'), parts along dimension 0
- y_target: bfloat16 [128, 256, 768], P('data'), parts along dimension 0
- w_up: bfloat16 [4, 768, 3072], P('stage')
- w_down: bfloat16 [4, 3072, 768], P('stage')
- gain: float32 [4, 768], P('stage')
Outputs:
- output 1: float32 [4], P('data'), parts along dimension 0
- output 2: float32 [16, 768, 3072], P(('data', 'stage')), parts along dimension 0
- output 3: float32 [16, 3072, 768], P(('data', 'stage')), parts along dimension 0
- output 4: float32 [16, 768], P(('data', 'stage')), parts along dimension 0
There are 4 independent parts. A program takes and returns all parts, laid end to end along the dimension named above; an argument that names none is the same for every part.
All inputs are finite; a program needn't handle non-finite values.
Results may differ from a plain program's by a relative error of at most 0.0053043.
Values are sent between devices in bfloat16 or wider.
A program may use at most 1 GiB of HBM per device.

v0:
```python
import jax
import jax.numpy as jnp
from jax import lax
from jax.sharding import PartitionSpec as P

NORM_EPS = 1e-6


def layer_forward(x_act, w_up, w_down, gain_vec):
    x_f = x_act.astype(jnp.float32)
    inv_rms = lax.rsqrt(jnp.mean(x_f * x_f, axis=-1, keepdims=True) + NORM_EPS)
    normed = (x_f * inv_rms * gain_vec).astype(jnp.bfloat16)
    pre_act = jnp.dot(normed, w_up, preferred_element_type=jnp.float32)
    hidden = jax.nn.gelu(pre_act).astype(jnp.bfloat16)
    update = jnp.dot(hidden, w_down, preferred_element_type=jnp.float32)
    return (x_f + update).astype(jnp.bfloat16)


def layer_backward(x_act, w_up, w_down, gain_vec, grad_out):
    x_f = x_act.astype(jnp.float32)
    inv_rms = lax.rsqrt(jnp.mean(x_f * x_f, axis=-1, keepdims=True) + NORM_EPS)
    x_hat = x_f * inv_rms
    normed = (x_hat * gain_vec).astype(jnp.bfloat16)
    pre_act = jnp.dot(normed, w_up, preferred_element_type=jnp.float32)
    hidden_f, gelu_pull = jax.vjp(jax.nn.gelu, pre_act)
    hidden = hidden_f.astype(jnp.bfloat16)
    grad_w_down = lax.dot_general(hidden, grad_out, (((0,), (0,)), ((), ())), preferred_element_type=jnp.float32)
    grad_hidden = lax.dot_general(grad_out, w_down, (((1,), (1,)), ((), ())), preferred_element_type=jnp.float32).astype(jnp.bfloat16)
    grad_pre = gelu_pull(grad_hidden.astype(jnp.float32))[0].astype(jnp.bfloat16)
    grad_w_up = lax.dot_general(normed, grad_pre, (((0,), (0,)), ((), ())), preferred_element_type=jnp.float32)
    grad_normed = lax.dot_general(grad_pre, w_up, (((1,), (1,)), ((), ())), preferred_element_type=jnp.float32).astype(jnp.bfloat16).astype(jnp.float32)
    grad_gain = jnp.sum(grad_normed * x_hat, axis=0)
    grad_hat = grad_normed * gain_vec
    grad_x = inv_rms * (grad_hat - x_hat * jnp.mean(grad_hat * x_hat, axis=-1, keepdims=True))
    grad_in = (grad_out.astype(jnp.float32) + grad_x).astype(jnp.bfloat16)
    return grad_in, grad_w_up, grad_w_down, grad_gain


def stage_forward(x_act, w_up, w_down, gain_rows):
    saved_list = []
    for layer_idx in range(w_up.shape[0]):
        saved_list.append(x_act)
        x_act = layer_forward(x_act, w_up[layer_idx], w_down[layer_idx], gain_rows[layer_idx])
    return x_act, jnp.stack(saved_list)


def stage_backward(saved_acts, w_up, w_down, gain_rows, grad_out):
    up_list = []
    down_list = []
    gain_list = []
    for layer_idx in reversed(range(w_up.shape[0])):
        grad_out, g_up, g_down, g_gain = layer_backward(saved_acts[layer_idx], w_up[layer_idx], w_down[layer_idx], gain_rows[layer_idx], grad_out)
        up_list.insert(0, g_up)
        down_list.insert(0, g_down)
        gain_list.insert(0, g_gain)
    return grad_out, jnp.stack(up_list), jnp.stack(down_list), jnp.stack(gain_list)


def solution(mesh):
    stages = mesh.shape["stage"]
    partner_perm = [(dev_pos, stages - 1 - dev_pos) for dev_pos in range(stages)]
    even_pairs = [(dev_pos, dev_pos ^ 1) for dev_pos in range(stages)]
    odd_pairs = [(dev_pos, dev_pos + 1 if dev_pos % 2 == 1 else dev_pos - 1) for dev_pos in range(1, stages - 1)]

    def device_step(x_in, y_target, w_up, w_down, gain):
        num_micro, tokens, model_width = x_in.shape
        half_micro = num_micro // 2
        lead_ticks = stages // 2 - 1
        loss_scale = 1.0 / (num_micro * tokens * model_width)
        stage_idx = lax.axis_index("stage")
        is_even = stage_idx % 2 == 0
        is_edge = (stage_idx == 0) | (stage_idx == stages - 1)
        own_sets = (w_up, w_down, gain)
        partner_sets = tuple(lax.ppermute(arr_w, "stage", partner_perm) for arr_w in own_sets)
        first_set = tuple(jnp.where(is_even, own_w, other_w) for own_w, other_w in zip(own_sets, partner_sets))
        second_set = tuple(jnp.where(is_even, other_w, own_w) for own_w, other_w in zip(own_sets, partner_sets))
        feed_rows = jnp.where(stage_idx == 0, x_in[:half_micro], x_in[half_micro:])
        target_rows = jnp.where(stage_idx == 0, y_target[half_micro:], y_target[:half_micro])
        pad_rows = jnp.zeros((lead_ticks, tokens, model_width), jnp.bfloat16)
        feed_rows = jnp.concatenate([feed_rows, pad_rows])
        zero_act = jnp.zeros((tokens, model_width), jnp.bfloat16)

        def forward_tick(recv_act, feed_row):
            first_out, first_saved = stage_forward(jnp.where(is_edge, feed_row, recv_act), first_set[0], first_set[1], first_set[2])
            passed = lax.ppermute(first_out, "stage", even_pairs)
            second_out, second_saved = stage_forward(passed, second_set[0], second_set[1], second_set[2])
            recv_next = lax.ppermute(second_out, "stage", odd_pairs)
            return recv_next, (first_saved, second_saved, second_out)

        _, (saved_first, saved_second, tick_outs) = lax.scan(forward_tick, zero_act, feed_rows)
        final_out = tick_outs[lead_ticks:lead_ticks + half_micro]
        delta_out = final_out.astype(jnp.float32) - target_rows.astype(jnp.float32)
        local_loss = jnp.where(is_edge, jnp.sum(delta_out * delta_out), 0.0) * loss_scale
        total_loss = lax.psum(local_loss, "stage")
        grad_final = jnp.where(is_edge, (2.0 * loss_scale) * delta_out, 0.0).astype(jnp.bfloat16)
        grad_feed = jnp.concatenate([pad_rows, grad_final])

        def backward_tick(bwd_carry, tick_in):
            recv_grad, acc_first, acc_second = bwd_carry
            saved_a, saved_b, feed_grad = tick_in
            mid_grad, up_b, down_b, gain_b = stage_backward(saved_b, second_set[0], second_set[1], second_set[2], jnp.where(is_edge, feed_grad, recv_grad))
            passed = lax.ppermute(mid_grad, "stage", even_pairs)
            first_grad, up_a, down_a, gain_a = stage_backward(saved_a, first_set[0], first_set[1], first_set[2], passed)
            recv_next = lax.ppermute(first_grad, "stage", odd_pairs)
            acc_first = (acc_first[0] + up_a, acc_first[1] + down_a, acc_first[2] + gain_a)
            acc_second = (acc_second[0] + up_b, acc_second[1] + down_b, acc_second[2] + gain_b)
            return (recv_next, acc_first, acc_second), None

        zero_set = (jnp.zeros(w_up.shape, jnp.float32), jnp.zeros(w_down.shape, jnp.float32), jnp.zeros(gain.shape, jnp.float32))
        (_, acc_first, acc_second), _ = lax.scan(backward_tick, (zero_act, zero_set, zero_set), (saved_first, saved_second, grad_feed), reverse=True)
        results = []
        for first_g, second_g in zip(acc_first, acc_second):
            own_part = jnp.where(is_even, first_g, second_g)
            partner_part = jnp.where(is_even, second_g, first_g)
            results.append(own_part + lax.ppermute(partner_part, "stage", partner_perm))
        return total_loss.reshape(1), results[0], results[1], results[2]

    weight_spec = P("stage", None, None)
    grad_spec = P(("data", "stage"), None, None)
    return jax.shard_map(device_step, mesh=mesh, in_specs=(P("data", None, None), P("data", None, None), weight_spec, weight_spec, P("stage", None)), out_specs=(P("data"), grad_spec, grad_spec, P(("data", "stage"), None)), check_vma=False)
```

profile of v0, /device:TPU:0, one launch (start us, length us, event | category | flops | bytes accessed | tf_op | source)
XLA Modules:
  0.0 2224.3 jit_solution(10443329056295320256)
XLA Ops:
  5.1 8.2 slice_select_fusion.1
  19.7 187.0 %collective-permute-done.4 = f32[1,768]{1,0:T(1,128)S(1)} collective-permute-done((f32[1,768]{1,0:T(1,128)}, f32[1,768]{1,0:T(1,128)S(1)}, u32[]{:S(2)}, u32[]{:S(2)}) %collective-permute-start.4) | collective-permute-done | bytes 3104 | tf_op jit(solution)/shard_map/ppermute | solution.py:74
  220.2 459.5 %while.44 = (s32[]{:T(128)}, bf16[256,768]{1,0:T(8,128)(2,1)S(1)}, bf16[17,1,256,768]{3,2,1,0:T(8,128)(2,1)}, bf16[17,1,256,768]{3,2,1,0:T(8,128)(2,1)}, bf16[17...) while((s32[]{:T(128)}, bf16[256,768]{1,0:T(8,128)(2,1)S(1)}, ...), condition=%wide.region_3.4_spmd, body=%wide.region_0.3_spmd.sunk | while | flops 4850123264 | bytes 27553528 | solution.py:90
  248.8 8.5 collective-permute-start
  276.7 8.0 collective-permute-start
  286.3 7.6 bitcast_dynamic-update-slice_fusion.7
  304.3 8.0 collective-permute-start
  331.7 8.0 collective-permute-start
  359.1 8.0 collective-permute-start
  386.6 8.0 collective-permute-start
  396.1 7.6 bitcast_dynamic-update-slice_fusion.7
  414.0 8.0 collective-permute-start
  423.6 7.6 bitcast_dynamic-update-slice_fusion.7
  441.5 8.0 collective-permute-start
  468.9 8.0 collective-permute-start
  478.4 7.6 bitcast_dynamic-update-slice_fusion.7
  496.4 8.0 collective-permute-start
  523.8 8.0 collective-permute-start
  551.2 8.0 collective-permute-start
  578.7 8.0 collective-permute-start
  606.2 8.0 collective-permute-start
  633.6 8.0 collective-permute-start
  661.0 8.0 collective-permute-start
  679.6 9.1 select_convert_fusion
  692.2 1088.2 %while.45 = (s32[]{:T(128)}, bf16[256,768]{1,0:T(8,128)(2,1)S(1)}, f32[1,768,3072]{2,1,0:T(8,128)}, f32[1,3072,768]{2,1,0:T(8,128)}, f32[1,768]{1,0:T(1,128)S(1)...) while((s32[]{:T(128)}, bf16[256,768]{1,0:T(8,128)(2,1)S(1)}, ...), condition=%wide.region_13.14_spmd.clone, body=%wide.region_6.13_spmd.clone.sunk | while | flops 12158830592 | bytes 425151424 | solution.py:110
  720.6 8.0 collective-permute-start.2
  729.8 8.0 bitcast_add_fusion.11
  790.9 10.8 bitcast_add_fusion.11
  853.1 10.8 bitcast_add_fusion.11
  916.9 10.8 bitcast_add_fusion.11
  979.1 10.8 bitcast_add_fusion.11
  1042.9 10.8 bitcast_add_fusion.11
  1105.1 10.8 bitcast_add_fusion.11
  1168.9 10.8 bitcast_add_fusion.11
  1231.1 10.8 bitcast_add_fusion.11
  1294.9 10.8 bitcast_add_fusion.11
  1357.1 10.8 bitcast_add_fusion.11
  1420.9 10.8 bitcast_add_fusion.11
  1483.1 10.8 bitcast_add_fusion.11
  1546.9 10.8 bitcast_add_fusion.11
  1609.1 10.8 bitcast_add_fusion.11
  1672.9 10.8 bitcast_add_fusion.11
  1735.1 10.8 bitcast_add_fusion.11
  1780.5 10.2 broadcast_select_fusion.5
  1792.4 8.4 broadcast_select_fusion.2
  1803.2 398.4 %psum.7 = f32[1]{0:T(128)} all-reduce(f32[1]{0:T(128)} %bitcast.8), channel_id=1, replica_groups=mesh['data'=4,'stage'=4] {'stage'}, use_global_device_ids=true, to_apply=%region_5.6 | all-reduce | flops 1 | bytes 8 | tf_op jit(solution)/shard_map/psum | solution.py:94
  2202.2 10.5 select_add_fusion.1
  2212.7 11.3 select_add_fusion
  (1513 shorter events, 1209.7 us)
Async XLA Ops:
  0.6 206.1 %collective-permute-start.5 = (bf16[1,768,3072]{2,1,0:T(8,128)(2,1)}, bf16[1,768,3072]{2,1,0:T(8,128)(2,1)}, u32[]{:S(2)}, u32[]{:S(2)}) collective-permute-start(bf16[1,768,3072]{2,1,0:T(8,128)(2,1)} %param.11), channel_id=1, source_target_pairs={{0,3},{1,2},{2,1},{3,0},{4,7},{5,6},{6,5},{7,4},{8,11},{9,10},{10,... | collective-permute-start | bytes 14155784 | tf_op jit(solution)/shard_map/ppermute | solution.py:74
  3.3 210.2 %collective-permute-start.6 = (bf16[1,3072,768]{2,1,0:T(8,128)(2,1)}, bf16[1,3072,768]{2,1,0:T(8,128)(2,1)}, u32[]{:S(2)}, u32[]{:S(2)}) collective-permute-start(bf16[1,3072,768]{2,1,0:T(8,128)(2,1)} %param.12), channel_id=1, source_target_pairs={{0,3},{1,2},{2,1},{3,0},{4,7},{5,6},{6,5},{7,4},{8,11},{9,10},{10,... | collective-permute-start | bytes 14155784 | tf_op jit(solution)/shard_map/ppermute | solution.py:74
  3.4 203.3 %collective-permute-start.4 = (f32[1,768]{1,0:T(1,128)}, f32[1,768]{1,0:T(1,128)S(1)}, u32[]{:S(2)}, u32[]{:S(2)}) collective-permute-start(f32[1,768]{1,0:T(1,128)} %param.13), channel_id=1, source_target_pairs={{0,3},{1,2},{2,1},{3,0},{4,7},{5,6},{6,5},{7,4},{8,11},{9,10},{10,... | collective-permute-start | bytes 9224 | tf_op jit(solution)/shard_map/ppermute | solution.py:74
  248.8 9.9 collective-permute-start
  276.7 9.4 collective-permute-start
  359.1 9.4 collective-permute-start
  414.0 9.4 collective-permute-start
  441.5 9.4 collective-permute-start
  523.8 9.4 collective-permute-start
  551.2 9.4 collective-permute-start
  578.7 9.4 collective-permute-start
  633.6 9.4 collective-permute-start
  661.0 9.4 collective-permute-start
  720.6 28.6 %collective-permute-start.2 = (bf16[256,768]{1,0:T(8,128)(2,1)}, bf16[256,768]{1,0:T(8,128)(2,1)S(1)}, u32[]{:S(2)}, u32[]{:S(2)}) collective-permute-start(bf16[256,768]{1,0:T(8,128)(2,1)} %fusion.277), channel_id=1, source_target_pairs={{0,1},{1,0},{2,3},{3,2},{4,5},{5,4},{6,7},{7,6},{8,9},{9,8},{10,11... | collective-permute-start | bytes 1179656 | tf_op jit(solution)/shard_map/while/body/eval_jaxpr/ppermute | solution.py:102
  786.8 26.3 %collective-permute-start.2 = (bf16[256,768]{1,0:T(8,128)(2,1)}, bf16[256,768]{1,0:T(8,128)(2,1)S(1)}, u32[]{:S(2)}, u32[]{:S(2)}) collective-permute-start(bf16[256,768]{1,0:T(8,128)(2,1)} %fusion.277), channel_id=1, source_target_pairs={{0,1},{1,0},{2,3},{3,2},{4,5},{5,4},{6,7},{7,6},{8,9},{9,8},{10,11... | collective-permute-start | bytes 1179656 | tf_op jit(solution)/shard_map/while/body/eval_jaxpr/ppermute | solution.py:102
  823.3 9.4 collective-permute-start.3
  850.6 24.6 %collective-permute-start.2 = (bf16[256,768]{1,0:T(8,128)(2,1)}, bf16[256,768]{1,0:T(8,128)(2,1)S(1)}, u32[]{:S(2)}, u32[]{:S(2)}) collective-permute-start(bf16[256,768]{1,0:T(8,128)(2,1)} %fusion.277), channel_id=1, source_target_pairs={{0,1},{1,0},{2,3},{3,2},{4,5},{5,4},{6,7},{7,6},{8,9},{9,8},{10,11... | collective-permute-start | bytes 1179656 | tf_op jit(solution)/shard_map/while/body/eval_jaxpr/ppermute | solution.py:102
  885.4 9.4 collective-permute-start.3
  912.8 26.3 %collective-permute-start.2 = (bf16[256,768]{1,0:T(8,128)(2,1)}, bf16[256,768]{1,0:T(8,128)(2,1)S(1)}, u32[]{:S(2)}, u32[]{:S(2)}) collective-permute-start(bf16[256,768]{1,0:T(8,128)(2,1)} %fusion.277), channel_id=1, source_target_pairs={{0,1},{1,0},{2,3},{3,2},{4,5},{5,4},{6,7},{7,6},{8,9},{9,8},{10,11... | collective-permute-start | bytes 1179656 | tf_op jit(solution)/shard_map/while/body/eval_jaxpr/ppermute | solution.py:102
  949.3 9.4 collective-permute-start.3
  976.6 24.6 %collective-permute-start.2 = (bf16[256,768]{1,0:T(8,128)(2,1)}, bf16[256,768]{1,0:T(8,128)(2,1)S(1)}, u32[]{:S(2)}, u32[]{:S(2)}) collective-permute-start(bf16[256,768]{1,0:T(8,128)(2,1)} %fusion.277), channel_id=1, source_target_pairs={{0,1},{1,0},{2,3},{3,2},{4,5},{5,4},{6,7},{7,6},{8,9},{9,8},{10,11... | collective-permute-start | bytes 1179656 | tf_op jit(solution)/shard_map/while/body/eval_jaxpr/ppermute | solution.py:102
  1011.4 9.4 collective-permute-start.3
  1038.8 26.3 %collective-permute-start.2 = (bf16[256,768]{1,0:T(8,128)(2,1)}, bf16[256,768]{1,0:T(8,128)(2,1)S(1)}, u32[]{:S(2)}, u32[]{:S(2)}) collective-permute-start(bf16[256,768]{1,0:T(8,128)(2,1)} %fusion.277), channel_id=1, source_target_pairs={{0,1},{1,0},{2,3},{3,2},{4,5},{5,4},{6,7},{7,6},{8,9},{9,8},{10,11... | collective-permute-start | bytes 1179656 | tf_op jit(solution)/shard_map/while/body/eval_jaxpr/ppermute | solution.py:102
  1075.3 9.4 collective-permute-start.3
  1102.6 24.6 %collective-permute-start.2 = (bf16[256,768]{1,0:T(8,128)(2,1)}, bf16[256,768]{1,0:T(8,128)(2,1)S(1)}, u32[]{:S(2)}, u32[]{:S(2)}) collective-permute-start(bf16[256,768]{1,0:T(8,128)(2,1)} %fusion.277), channel_id=1, source_target_pairs={{0,1},{1,0},{2,3},{3,2},{4,5},{5,4},{6,7},{7,6},{8,9},{9,8},{10,11... | collective-permute-start | bytes 1179656 | tf_op jit(solution)/shard_map/while/body/eval_jaxpr/ppermute | solution.py:102
  1137.4 9.4 collective-permute-start.3
  1164.8 26.3 %collective-permute-start.2 = (bf16[256,768]{1,0:T(8,128)(2,1)}, bf16[256,768]{1,0:T(8,128)(2,1)S(1)}, u32[]{:S(2)}, u32[]{:S(2)}) collective-permute-start(bf16[256,768]{1,0:T(8,128)(2,1)} %fusion.277), channel_id=1, source_target_pairs={{0,1},{1,0},{2,3},{3,2},{4,5},{5,4},{6,7},{7,6},{8,9},{9,8},{10,11... | collective-permute-start | bytes 1179656 | tf_op jit(solution)/shard_map/while/body/eval_jaxpr/ppermute | solution.py:102
  1201.2 9.4 collective-permute-start.3
  1228.6 24.6 %collective-permute-start.2 = (bf16[256,768]{1,0:T(8,128)(2,1)}, bf16[256,768]{1,0:T(8,128)(2,1)S(1)}, u32[]{:S(2)}, u32[]{:S(2)}) collective-permute-start(bf16[256,768]{1,0:T(8,128)(2,1)} %fusion.277), channel_id=1, source_target_pairs={{0,1},{1,0},{2,3},{3,2},{4,5},{5,4},{6,7},{7,6},{8,9},{9,8},{10,11... | collective-permute-start | bytes 1179656 | tf_op jit(solution)/shard_map/while/body/eval_jaxpr/ppermute | solution.py:102
  1263.4 9.4 collective-permute-start.3
  1290.7 26.3 %collective-permute-start.2 = (bf16[256,768]{1,0:T(8,128)(2,1)}, bf16[256,768]{1,0:T(8,128)(2,1)S(1)}, u32[]{:S(2)}, u32[]{:S(2)}) collective-permute-start(bf16[256,768]{1,0:T(8,128)(2,1)} %fusion.277), channel_id=1, source_target_pairs={{0,1},{1,0},{2,3},{3,2},{4,5},{5,4},{6,7},{7,6},{8,9},{9,8},{10,11... | collective-permute-start | bytes 1179656 | tf_op jit(solution)/shard_map/while/body/eval_jaxpr/ppermute | solution.py:102
  1327.2 9.4 collective-permute-start.3
  1354.6 24.6 %collective-permute-start.2 = (bf16[256,768]{1,0:T(8,128)(2,1)}, bf16[256,768]{1,0:T(8,128)(2,1)S(1)}, u32[]{:S(2)}, u32[]{:S(2)}) collective-permute-start(bf16[256,768]{1,0:T(8,128)(2,1)} %fusion.277), channel_id=1, source_target_pairs={{0,1},{1,0},{2,3},{3,2},{4,5},{5,4},{6,7},{7,6},{8,9},{9,8},{10,11... | collective-permute-start | bytes 1179656 | tf_op jit(solution)/shard_map/while/body/eval_jaxpr/ppermute | solution.py:102
  1389.4 9.4 collective-permute-start.3
  1416.7 26.3 %collective-permute-start.2 = (bf16[256,768]{1,0:T(8,128)(2,1)}, bf16[256,768]{1,0:T(8,128)(2,1)S(1)}, u32[]{:S(2)}, u32[]{:S(2)}) collective-permute-start(bf16[256,768]{1,0:T(8,128)(2,1)} %fusion.277), channel_id=1, source_target_pairs={{0,1},{1,0},{2,3},{3,2},{4,5},{5,4},{6,7},{7,6},{8,9},{9,8},{10,11... | collective-permute-start | bytes 1179656 | tf_op jit(solution)/shard_map/while/body/eval_jaxpr/ppermute | solution.py:102
  1453.2 9.4 collective-permute-start.3
  1480.6 24.6 %collective-permute-start.2 = (bf16[256,768]{1,0:T(8,128)(2,1)}, bf16[256,768]{1,0:T(8,128)(2,1)S(1)}, u32[]{:S(2)}, u32[]{:S(2)}) collective-permute-start(bf16[256,768]{1,0:T(8,128)(2,1)} %fusion.277), channel_id=1, source_target_pairs={{0,1},{1,0},{2,3},{3,2},{4,5},{5,4},{6,7},{7,6},{8,9},{9,8},{10,11... | collective-permute-start | bytes 1179656 | tf_op jit(solution)/shard_map/while/body/eval_jaxpr/ppermute | solution.py:102
  1515.4 9.4 collective-permute-start.3
  1542.7 26.3 %collective-permute-start.2 = (bf16[256,768]{1,0:T(8,128)(2,1)}, bf16[256,768]{1,0:T(8,128)(2,1)S(1)}, u32[]{:S(2)}, u32[]{:S(2)}) collective-permute-start(bf16[256,768]{1,0:T(8,128)(2,1)} %fusion.277), channel_id=1, source_target_pairs={{0,1},{1,0},{2,3},{3,2},{4,5},{5,4},{6,7},{7,6},{8,9},{9,8},{10,11... | collective-permute-start | bytes 1179656 | tf_op jit(solution)/shard_map/while/body/eval_jaxpr/ppermute | solution.py:102
  1579.2 9.4 collective-permute-start.3
  1606.6 24.6 %collective-permute-start.2 = (bf16[256,768]{1,0:T(8,128)(2,1)}, bf16[256,768]{1,0:T(8,128)(2,1)S(1)}, u32[]{:S(2)}, u32[]{:S(2)}) collective-permute-start(bf16[256,768]{1,0:T(8,128)(2,1)} %fusion.277), channel_id=1, source_target_pairs={{0,1},{1,0},{2,3},{3,2},{4,5},{5,4},{6,7},{7,6},{8,9},{9,8},{10,11... | collective-permute-start | bytes 1179656 | tf_op jit(solution)/shard_map/while/body/eval_jaxpr/ppermute | solution.py:102
  1641.4 9.4 collective-permute-start.3
  1668.7 26.3 %collective-permute-start.2 = (bf16[256,768]{1,0:T(8,128)(2,1)}, bf16[256,768]{1,0:T(8,128)(2,1)S(1)}, u32[]{:S(2)}, u32[]{:S(2)}) collective-permute-start(bf16[256,768]{1,0:T(8,128)(2,1)} %fusion.277), channel_id=1, source_target_pairs={{0,1},{1,0},{2,3},{3,2},{4,5},{5,4},{6,7},{7,6},{8,9},{9,8},{10,11... | collective-permute-start | bytes 1179656 | tf_op jit(solution)/shard_map/while/body/eval_jaxpr/ppermute | solution.py:102
  1705.2 9.4 collective-permute-start.3
  1732.6 24.6 %collective-permute-start.2 = (bf16[256,768]{1,0:T(8,128)(2,1)}, bf16[256,768]{1,0:T(8,128)(2,1)S(1)}, u32[]{:S(2)}, u32[]{:S(2)}) collective-permute-start(bf16[256,768]{1,0:T(8,128)(2,1)} %fusion.277), channel_id=1, source_target_pairs={{0,1},{1,0},{2,3},{3,2},{4,5},{5,4},{6,7},{7,6},{8,9},{9,8},{10,11... | collective-permute-start | bytes 1179656 | tf_op jit(solution)/shard_map/while/body/eval_jaxpr/ppermute | solution.py:102
  1790.7 411.6 %collective-permute-start.7 = (f32[1,768,3072]{2,1,0:T(8,128)}, f32[1,768,3072]{2,1,0:T(8,128)}, u32[]{:S(2)}, u32[]{:S(2)}) collective-permute-start(f32[1,768,3072]{2,1,0:T(8,128)} %broadcast_select_fusion.5), channel_id=1, source_target_pairs={{0,3},{1,2},{2,1},{3,0},{4,7},{5,6},{6,5},{7,4},{8,11},{9,10},{10,... | collective-permute-start | bytes 28311560 | tf_op jit(solution)/shard_map/ppermute | solution.py:115
  1800.8 411.9 %collective-permute-start.8 = (f32[1,3072,768]{2,1,0:T(8,128)}, f32[1,3072,768]{2,1,0:T(8,128)}, u32[]{:S(2)}, u32[]{:S(2)}) collective-permute-start(f32[1,3072,768]{2,1,0:T(8,128)} %broadcast_select_fusion.2), channel_id=1, source_target_pairs={{0,3},{1,2},{2,1},{3,0},{4,7},{5,6},{6,5},{7,4},{8,11},{9,10},{10,... | collective-permute-start | bytes 28311560 | tf_op jit(solution)/shard_map/ppermute | solution.py:115
  1800.8 400.8 %collective-permute-start.9 = (f32[1,768]{1,0:T(1,128)S(1)}, f32[1,768]{1,0:T(1,128)S(1)}, u32[]{:S(2)}, u32[]{:S(2)}) collective-permute-start(f32[1,768]{1,0:T(1,128)S(1)} %broadcast_select_fusion.8), channel_id=1, source_target_pairs={{0,3},{1,2},{2,1},{3,0},{4,7},{5,6},{6,5},{7,4},{8,11},{9,10},{10,... | collective-permute-start | bytes 9224 | tf_op jit(solution)/shard_map/ppermute | solution.py:115
  (387 other events, 3292.4 us)
where the time goes:
time: 2230 us; the launch traced here: 2220 us
  matrix products  1050 us (47%)
  blocking collectives  398 us (18%)
  other arithmetic  228 us (10%)
  waiting for transfers between devices  210 us (9%)
  starting transfers between devices  202 us (9%)
  local copies, waits for them, and re-layouts  117 us (5%)
    psum x1, blocking collectives, device_step(): total_loss = lax.psum(local_loss, 'stage')  398 us
    dot_general x34, matrix products, layer_backward(): lax.dot_general(hidden, grad_out, (((0,), (0,)), ((), ())), preferred_ele...  253 us
    dot_general x34, matrix products, layer_forward(): update = jnp.dot(hidden, w_down, preferred_element_type=jnp.float32)  245 us
    dot_general x34, matrix products, layer_backward(): pre_act = jnp.dot(normed, w_up, preferred_element_type=jnp.float32)  194 us
    ppermute x3, waiting for transfers between devices, device_step(): lax.ppermute(arr_w, 'stage', partner_perm)  187 us
    dot_general x34, matrix products, layer_backward(): lax.dot_general(normed, grad_pre, (((0,), (0,)), ((), ())), preferred_ele...  140 us
    ppermute x17, starting transfers between devices, forward_tick(): passed = lax.ppermute(first_out, 'stage', even_pairs)  129 us
    dot_general x34, matrix products, layer_backward(): lax.dot_general(grad_pre, w_up, (((1,), (1,)), ((), ())), preferred_eleme...  114 us
  transfers between devices with their start and end apart: 74, of which 18 were waited for; matrix products, arithmetic and copies ran while one was open for 27% of the time, Pallas kernels for 0%

commit v1 on v0

v1 whole, which is shorter than its diff:
```python
import functools

import jax
import jax.numpy as jnp
from jax import lax
from jax.experimental import pallas as pl
from jax.experimental.pallas import tpu as pltpu
from jax.sharding import PartitionSpec as P

MESH = pl.DeviceIdType.MESH
F32 = jnp.float32
BF16 = jnp.bfloat16
NORM_EPS = 1e-6
STAGES = 4
LAG = 3
RING = 12
COLS = 512
ROWS = 64
NT = (((1,), (1,)), ((), ()))
GELU_C = 0.7978845608028654
GELU_A = 0.044715


def pipeline_kernel(x_hbm, y_hbm, w1_hbm, w2_hbm, gain_ref,
                    n_hbm, a_hbm, du_hbm, g_hbm, d_hbm, gg_ref, loss_ref,
                    w1, w2, xring, gring, xsend, gsend, nbuf, abuf, dbuf, dubuf, ybuf, gnbuf, lbuf,
                    wsem, xrecv, grecv, xsem, gsem, nsem, asem, dosem, dusem, ghsem, disem, ysem, lsend, lrecv):
    micro, tokens, width = x_hbm.shape
    hidden = w1.shape[1]
    stage = lax.axis_index("stage")
    first = stage == 0
    last = stage == STAGES - 1
    lag = LAG * (STAGES - 1 - stage)
    scale = 1.0 / (micro * tokens * width)

    def at_stage(pos):
        return {"stage": pos}

    def copy_w1():
        return pltpu.make_async_copy(w1_hbm.at[0], w1, wsem.at[0])

    def copy_w2():
        return pltpu.make_async_copy(w2_hbm.at[0], w2, wsem.at[1])

    def load_x(i):
        slot = lax.rem(i, RING)
        return pltpu.make_async_copy(x_hbm.at[i], xring.at[slot], xrecv.at[slot])

    def load_y(i):
        return pltpu.make_async_copy(y_hbm.at[i], ybuf.at[lax.rem(i, 2)], ysem.at[lax.rem(i, 2)])

    def send_x(i):
        return pltpu.make_async_remote_copy(
            src_ref=xsend.at[lax.rem(i, 2)], dst_ref=xring.at[lax.rem(i, RING)], send_sem=xsem.at[lax.rem(i, 2)],
            recv_sem=xrecv.at[lax.rem(i, RING)], device_id=at_stage(lax.rem(stage + 1, STAGES)), device_id_type=MESH)

    def send_g(i):
        return pltpu.make_async_remote_copy(
            src_ref=gsend.at[lax.rem(i, 2)], dst_ref=gring.at[lax.rem(i, RING)], send_sem=gsem.at[lax.rem(i, 2)],
            recv_sem=grecv.at[lax.rem(i, RING)], device_id=at_stage(lax.rem(stage + STAGES - 1, STAGES)),
            device_id_type=MESH)

    def save_n(i):
        return pltpu.make_async_copy(nbuf.at[lax.rem(i, 2)], n_hbm.at[i], nsem.at[lax.rem(i, 2)])

    def save_a(i):
        return pltpu.make_async_copy(abuf.at[lax.rem(i, 2)], a_hbm.at[i], asem.at[lax.rem(i, 2)])

    def save_d(i):
        return pltpu.make_async_copy(dbuf.at[lax.rem(i, 2)], d_hbm.at[i], dosem.at[lax.rem(i, 2)])

    def load_d(i):
        return pltpu.make_async_copy(d_hbm.at[i], dbuf.at[2 + lax.rem(i, 2)], disem.at[lax.rem(i, 2)])

    def save_du(i):
        return pltpu.make_async_copy(dubuf.at[lax.rem(i, 2)], du_hbm.at[i], dusem.at[lax.rem(i, 2)])

    def save_g(i):
        return pltpu.make_async_copy(gring.at[lax.rem(i, RING)], g_hbm.at[i], ghsem)

    copy_w1().start()
    copy_w2().start()

    @pl.when(first)
    def _():
        load_x(0).start()

    @pl.when(last)
    def _():
        load_y(0).start()

    barrier = pltpu.get_barrier_semaphore()
    for step in range(1, STAGES):
        pl.semaphore_signal(barrier, inc=1, device_id=at_stage(lax.rem(stage + step, STAGES)), device_id_type=MESH)
    pl.semaphore_wait(barrier, STAGES - 1)

    gg_ref[...] = jnp.zeros_like(gg_ref)
    lbuf[...] = jnp.zeros_like(lbuf)
    copy_w1().wait()
    copy_w2().wait()

    def forward(i):
        slot = lax.rem(i, RING)
        two = lax.rem(i, 2)

        @pl.when(first)
        def _():
            load_x(i).wait()

            @pl.when(i + 1 < micro)
            def _():
                load_x(i + 1).start()

        @pl.when(jnp.logical_not(first))
        def _():
            send_x(i).wait_recv()

        gain = gain_ref[...]
        for row in range(0, tokens, ROWS):
            x_f = xring[slot, row:row + ROWS, :].astype(F32)
            inv = lax.rsqrt(jnp.mean(x_f * x_f, axis=-1, keepdims=True) + NORM_EPS)
            nbuf[two, row:row + ROWS, :] = (x_f * inv * gain).astype(BF16)
        save_n(i).start()
        for col in range(0, hidden, COLS):
            u = jnp.dot(nbuf[two], w1[:, col:col + COLS], preferred_element_type=F32)
            u_sq = u * u
            th = jnp.tanh(u * (GELU_C + (GELU_C * GELU_A) * u_sq))
            h = 0.5 * th + 0.5
            abuf[two, :, col:col + COLS] = (u * h).astype(BF16)
            slope = u * (2.0 * GELU_C + (6.0 * GELU_C * GELU_A) * u_sq)
            dbuf[two, :, col:col + COLS] = h + (h - h * h) * slope
        save_a(i).start()

        @pl.when(jnp.logical_not(last))
        def _():
            save_d(i).start()

        update = jnp.dot(abuf[two], w2[...], preferred_element_type=F32)
        xsend[two] = (xring[slot].astype(F32) + update).astype(BF16)

        @pl.when(jnp.logical_not(last))
        def _():
            send_x(i).start()

        @pl.when(last)
        def _():
            load_y(i).wait()

            @pl.when(i + 1 < micro)
            def _():
                load_y(i + 1).start()

            for row in range(0, tokens, ROWS):
                delta = xsend[two, row:row + ROWS, :].astype(F32) - ybuf[two, row:row + ROWS, :].astype(F32)
                gring[slot, row:row + ROWS, :] = ((2.0 * scale) * delta).astype(BF16)
                lbuf[...] += jnp.sum((delta * delta).reshape(ROWS // 8, 8, width), axis=0)

    def backward(j):
        slot = lax.rem(j, RING)
        two = lax.rem(j, 2)
        d_slot = jnp.where(last, two, 2 + two)

        @pl.when(jnp.logical_not(last))
        def _():
            load_d(j).wait()
            send_g(j).wait_recv()

        save_g(j).start()
        for col in range(0, hidden, COLS):
            ga = lax.dot_general(gring[slot], w2[col:col + COLS, :], NT, preferred_element_type=F32)
            ga = ga.astype(BF16).astype(F32)
            dubuf[two, :, col:col + COLS] = (ga * dbuf[d_slot, :, col:col + COLS]).astype(BF16)
        save_du(j).start()
        gnbuf[...] = lax.dot_general(dubuf[two], w1[...], NT, preferred_element_type=F32).astype(BF16)
        gain = gain_ref[...]
        for row in range(0, tokens, ROWS):
            x_f = xring[slot, row:row + ROWS, :].astype(F32)
            inv = lax.rsqrt(jnp.mean(x_f * x_f, axis=-1, keepdims=True) + NORM_EPS)
            x_hat = x_f * inv
            gn = gnbuf[row:row + ROWS, :].astype(F32)
            gg_ref[...] += jnp.sum((gn * x_hat).reshape(ROWS // 8, 8, width), axis=0)
            ghat = gn * gain
            gx = inv * (ghat - x_hat * jnp.mean(ghat * x_hat, axis=-1, keepdims=True))
            gsend[two, row:row + ROWS, :] = (gring[slot, row:row + ROWS, :].astype(F32) + gx).astype(BF16)

        @pl.when(jnp.logical_not(first))
        def _():
            send_g(j).start()

    def tick(t, carry):
        i = t
        j = t - lag

        @pl.when((i >= 2) & (i < micro + 2))
        def _():
            save_n(i - 2).wait()
            save_a(i - 2).wait()

            @pl.when(jnp.logical_not(last))
            def _():
                save_d(i - 2).wait()
                send_x(i - 2).wait_send()

        @pl.when((j >= 1) & (j < micro + 1))
        def _():
            save_g(j - 1).wait()

        @pl.when((j >= 2) & (j < micro + 2))
        def _():
            save_du(j - 2).wait()

            @pl.when(jnp.logical_not(first))
            def _():
                send_g(j - 2).wait_send()

        @pl.when(i < micro)
        def _():
            forward(i)

        @pl.when(jnp.logical_not(last) & (j + 1 >= 0) & (j + 1 < micro))
        def _():
            load_d(j + 1).start()

        @pl.when((j >= 0) & (j < micro))
        def _():
            backward(j)

        return carry

    lax.fori_loop(0, micro + LAG * (STAGES - 1) + 2, tick, 0)

    def send_loss(pos):
        return pltpu.make_async_remote_copy(
            src_ref=lbuf, dst_ref=lbuf, send_sem=lsend.at[pos], recv_sem=lrecv, device_id=at_stage(pos),
            device_id_type=MESH)

    @pl.when(last)
    def _():
        for pos in range(STAGES - 1):
            send_loss(pos).start()
        for pos in range(STAGES - 1):
            send_loss(pos).wait_send()

    @pl.when(jnp.logical_not(last))
    def _():
        send_loss(0).wait_recv()

    loss_ref[...] = lbuf[...]


def run_pipeline(x_in, y_target, w_up, w_down, gain):
    micro, tokens, width = x_in.shape
    hidden = w_up.shape[2]
    any_spec = pl.BlockSpec(memory_space=pl.ANY)
    vmem_spec = pl.BlockSpec(memory_space=pltpu.VMEM)
    dma = pltpu.SemaphoreType.DMA
    return pl.pallas_call(
        pipeline_kernel,
        out_shape=(
            jax.ShapeDtypeStruct((micro, tokens, width), BF16),
            jax.ShapeDtypeStruct((micro, tokens, hidden), BF16),
            jax.ShapeDtypeStruct((micro, tokens, hidden), BF16),
            jax.ShapeDtypeStruct((micro, tokens, width), BF16),
            jax.ShapeDtypeStruct((micro, tokens, hidden), F32),
            jax.ShapeDtypeStruct((8, width), F32),
            jax.ShapeDtypeStruct((8, width), F32),
        ),
        in_specs=[any_spec, any_spec, any_spec, any_spec, vmem_spec],
        out_specs=(any_spec, any_spec, any_spec, any_spec, any_spec, vmem_spec, vmem_spec),
        scratch_shapes=[
            pltpu.VMEM((width, hidden), BF16),
            pltpu.VMEM((hidden, width), BF16),
            pltpu.VMEM((RING, tokens, width), BF16),
            pltpu.VMEM((RING, tokens, width), BF16),
            pltpu.VMEM((2, tokens, width), BF16),
            pltpu.VMEM((2, tokens, width), BF16),
            pltpu.VMEM((2, tokens, width), BF16),
            pltpu.VMEM((2, tokens, hidden), BF16),
            pltpu.VMEM((4, tokens, hidden), F32),
            pltpu.VMEM((2, tokens, hidden), BF16),
            pltpu.VMEM((2, tokens, width), BF16),
            pltpu.VMEM((tokens, width), BF16),
            pltpu.VMEM((8, width), F32),
            dma((2,)), dma((RING,)), dma((RING,)), dma((2,)), dma((2,)), dma((2,)), dma((2,)), dma((2,)), dma((2,)),
            dma, dma((2,)), dma((2,)), dma((STAGES - 1,)), dma,
        ],
        compiler_params=pltpu.CompilerParams(
            collective_id=0, has_side_effects=True, vmem_limit_bytes=67043328),
        cost_estimate=pl.CostEstimate(
            flops=8 * micro * tokens * width * hidden, transcendentals=micro * tokens * hidden,
            bytes_accessed=16 * micro * tokens * hidden),
        name="pipeline",
    )(x_in, y_target, w_up, w_down, gain)


def solution(mesh):
    def device_step(x_in, y_target, w_up, w_down, gain):
        micro, tokens, width = x_in.shape
        hidden = w_up.shape[2]
        n_all, a_all, du_all, g_all, _, gain_rows, loss_rows = run_pipeline(x_in, y_target, w_up, w_down, gain)
        rows = micro * tokens
        contract = (((0,), (0,)), ((), ()))
        grad_up = lax.dot_general(n_all.reshape(rows, width), du_all.reshape(rows, hidden), contract,
                                  preferred_element_type=F32)
        grad_down = lax.dot_general(a_all.reshape(rows, hidden), g_all.reshape(rows, width), contract,
                                    preferred_element_type=F32)
        loss = jnp.sum(loss_rows) * (1.0 / (rows * width))
        grad_gain = jnp.sum(gain_rows, axis=0, keepdims=True)
        return loss.reshape(1), grad_up[None], grad_down[None], grad_gain

    weight_spec = P("stage", None, None)
    grad_spec = P(("data", "stage"), None, None)
    return jax.shard_map(
        device_step, mesh=mesh,
        in_specs=(P("data", None, None), P("data", None, None), weight_spec, weight_spec, P("stage", None)),
        out_specs=(P("data"), grad_spec, grad_spec, P(("data", "stage"), None)), check_vma=False)
```

time: 2230 us -> 365 us (0.16)
  matrix products: 1050 us -> 94.1 us
  blocking collectives: 398 us -> 0 us
  Pallas kernels: 0 us -> 266 us
  other arithmetic: 228 us -> 2.1 us
  waiting for transfers between devices: 210 us -> 0 us
  starting transfers between devices: 202 us -> 0 us
  local copies, waits for them, and re-layouts: 117 us -> 0.58 us
    dot_general x204 -> x2, matrix products: 1050 us -> 94.1 us  [the longest x1 48.3 us: device_step(): lax.dot_general(n_all.reshape(rows, width), du_all.reshape(rows, hidden),...]
    psum x1 -> x0, blocking collectives: 398 us -> none  [device_step(): total_loss = lax.psum(local_loss, 'stage')]
    pallas_call x0 -> x1, Pallas kernels: none -> 266 us  [run_pipeline(): pl.pallas_call(pipeline_kernel, out_shape=(jax.ShapeDtypeStruct((micro, t...]
    ppermute x74 -> x0, waiting for transfers between devices: 210 us -> none  [the longest x3 187 us: device_step(): lax.ppermute(arr_w, 'stage', partner_perm)]
    ppermute x74 -> x0, starting transfers between devices: 202 us -> none  [the longest x17 129 us: forward_tick(): passed = lax.ppermute(first_out, 'stage', even_pairs)]
    while x714 -> x0, local copies, waits for them, and re-layouts: 93.2 us -> none
    convert_element_type x35 -> x0, other arithmetic: 66.8 us -> none  [the longest x34 57.8 us: layer_backward(): grad_in = (grad_out.astype(jnp.float32) + grad_x).astype(jnp.bfloat16)]
    select_n x24 -> x0, other arithmetic: 60.5 us -> none  [the longest x17 20.3 us: backward_tick(): jnp.where(is_edge, feed_grad, recv_grad)]
  transfers between devices with their start and end apart: 74 -> 0, of which waited for: 18 -> 0; matrix products, arithmetic and copies ran while one was open for 27% -> 0% of each run, Pallas kernels for 0% -> 0%
where the time goes in v1:
time: 365 us
  Pallas kernels  266 us (73%)
  matrix products  94.1 us (26%)
    pallas_call x1, Pallas kernels, run_pipeline(): pl.pallas_call(pipeline_kernel, out_shape=(jax.ShapeDtypeStruct((micro, t...  266 us
    dot_general x1, matrix products, device_step(): lax.dot_general(n_all.reshape(rows, width), du_all.reshape(rows, hidden),...  48.3 us
    dot_general x1, matrix products, device_step(): lax.dot_general(a_all.reshape(rows, hidden), g_all.reshape(rows, width),...  45.7 us

profile of v1, /device:TPU:0, one launch (start us, length us, event | category | flops | bytes accessed | tf_op | source)
XLA Modules:
  0.0 364.7 jit_solution(8842734977856596627)
XLA Ops:
  0.6 265.5 %pipeline.1 = (bf16[32,256,768]{2,1,0:T(8,128)(2,1)}, bf16[32,256,3072]{2,1,0:T(8,128)(2,1)}, bf16[32,256,3072]{2,1,0:T(8,128)(2,1)}, bf16[32,256,768]{2,1,0:T(8...) custom-call(bf16[32,256,768]{2,1,0:T(8,128)(2,1)} %x_hbm.1, ...), custom_call_target="tpu_custom_call" | custom-call | flops 154618822656 | bytes 402653184 | tf_op jit(solution)/shard_map/pipeline/pallas_call | solution.py:257
  266.2 1.3 reduce_sum.18
  268.2 0.8 reduce_sum.19
  268.9 0.6 broadcast_in_dim.11
  269.5 0.0 copy-start
  269.5 48.3 %convolution_bitcast_fusion.1 = f32[1,768,3072]{2,1,0:T(8,128)} fusion(bf16[32,256,768]{2,1,0:T(8,128)(2,1)} %get-tuple-element.11, bf16[32,256,3072]{2,1,0:T(8,128)(2,1)} %get-tuple-element.12), kind=kOutput, calls=%fused_computation.1 | convolution fusion | flops 38654705664 | bytes 72351744 | tf_op jit(solution)/shard_map/dot_general | solution.py:303
  317.9 0.0 copy-done
  317.9 45.7 %convolution_bitcast_fusion = f32[1,3072,768]{2,1,0:T(8,128)} fusion(bf16[32,256,3072]{2,1,0:T(8,128)(2,1)} %get-tuple-element.13, bf16[32,256,768]{2,1,0:T(8,128)(2,1)S(1)} %copy-done), kind=kOutput, calls=%fused_computation | convolution fusion | flops 38654705664 | bytes 72351744 | tf_op jit(solution)/shard_map/dot_general | solution.py:305
Async XLA Ops:
  269.5 48.3 %copy-start = (bf16[32,256,768]{2,1,0:T(8,128)(2,1)S(1)}, bf16[32,256,768]{2,1,0:T(8,128)(2,1)}, u32[]{:S(2)}) copy-start(bf16[32,256,768]{2,1,0:T(8,128)(2,1)} %get-tuple-element.14) | copy-start | bytes 37748740
